TPU v7x, 512 devices: a whole 4x8x8 slice. The times are simulated.
512 devices in a mesh: section: 32 (over x, y_hi, core), dp: 16 (over y_lo, z).
Axes of the slice: x: 4, y: 8 (y_hi: 4, y_lo: 2; y = y_hi * 2 + y_lo), z: 8, core: 2. Of those that a mesh axis runs over, the one named last changes fastest.
Arguments:
- out_pair: float32 [2048, 2048], P('dp'), may hold values from -6 to 6
- out_grad: bfloat16 [2048, 2048], P('dp'), may hold values from -6 to 6
- f_weight: bfloat16 [32, 1024, 1024], P('section', 'dp'), may hold values from -0.09375 to 0.09375
- g_weight: bfloat16 [32, 1024, 1024], P('section', 'dp'), may hold values from -0.09375 to 0.09375
- gains: float32 [32, 2, 1024], P('section'), may hold values from 0.1 to 1.9
Outputs:
- in_pair: float32 [32, 2048, 2048], P('section', 'dp')
- in_grad: bfloat16 [32, 2048, 2048], P('section', 'dp')
- f_grad: float32 [32, 1024, 1024], P('section', 'dp')
- g_grad: float32 [32, 1024, 1024], P('section', 'dp')
- gains_grad: float32 [32, 2, 1024], P('section')
All inputs are finite; a program needn't handle non-finite values.
Results may differ from a plain program's by a relative error of at most 0.04.
Values may be sent and summed in bfloat16 or wider, within the bound.
A program may use at most 64 MiB of HBM per device.

v0:
```python
import jax
import jax.numpy as jnp
from jax import lax
from jax.sharding import PartitionSpec as P

offset = 0.25


def in_one_piece(arrays, axis, dim, along):
    widths = [a.shape[along] for a in arrays]
    both = jnp.concatenate(arrays, axis=along)
    result = lax.all_gather(both, axis, axis=dim, tiled=True)
    return tuple(jnp.split(result, [sum(widths[:k]) for k in range(1, len(widths))], axis=along))


def from_behind(array, axis, by):
    devices = lax.axis_size(axis)
    pairs = [(i, i + by) for i in range(devices) if 0 <= i + by < devices]
    return lax.ppermute(array, axis, pairs)


def sent_together(arrays, axis, dim, along):
    ends, at = ([], 0)
    for a in arrays[:-1]:
        at += a.shape[along]
        ends.append(at)
    both = jnp.concatenate(arrays, axis=along)
    return tuple(
        jnp.split(lax.psum_scatter(both, axis, scatter_dimension=dim, tiled=True), ends, axis=along)
    )


def silu_parts(pre_values):
    sigmoid_value = jax.nn.sigmoid(pre_values)
    return (pre_values * sigmoid_value, sigmoid_value * (1.0 + pre_values * (1.0 - sigmoid_value)))


def normalize(values, gain_row):
    inv_scale = lax.rsqrt(jnp.mean(values * values, axis=-1, keepdims=True) + offset)
    return ((values * inv_scale * gain_row).astype(jnp.bfloat16), inv_scale)


def norm_back(values, inv_scale, gain_row, upstream):
    weighted = gain_row * upstream
    cubed = inv_scale * inv_scale * inv_scale
    return inv_scale * weighted - values * cubed * jnp.mean(
        weighted * values, axis=-1, keepdims=True
    )


def times_transposed(delta, weight_full):
    return lax.dot_general(
        delta, weight_full, (((1,), (1,)), ((), ())), preferred_element_type=jnp.float32
    )


def coupling_back(upper_out, lower_out, upper_grad, lower_grad, w_first, w_second, gain_pair):
    normed_second, scale_second = normalize(upper_out, gain_pair[1])
    pre_second = jnp.dot(normed_second, w_second, preferred_element_type=jnp.float32)
    act_second, slope_second = silu_parts(pre_second)
    lower_in = lower_out - act_second
    normed_first, scale_first = normalize(lower_in, gain_pair[0])
    pre_first = jnp.dot(normed_first, w_first, preferred_element_type=jnp.float32)
    act_first, slope_first = silu_parts(pre_first)
    upper_in = upper_out - act_first
    delta_second = (lower_grad * slope_second).astype(jnp.bfloat16)
    back_second = times_transposed(delta_second, w_second)
    through = upper_grad + norm_back(upper_out, scale_second, gain_pair[1], back_second)
    delta_first = (through * slope_first).astype(jnp.bfloat16)
    back_first = times_transposed(delta_first, w_first)
    lower_total = lower_grad + norm_back(lower_in, scale_first, gain_pair[0], back_first)
    gain_terms = jnp.stack(
        [
            jnp.sum(back_first * lower_in * scale_first, axis=0),
            jnp.sum(back_second * upper_out * scale_second, axis=0),
        ]
    )
    return (
        upper_in,
        lower_in,
        through.astype(jnp.bfloat16),
        lower_total.astype(jnp.bfloat16),
        normed_first,
        delta_first,
        normed_second,
        delta_second,
        gain_terms,
    )


def shards(out_pair, out_grad, f_weight, g_weight, gains):
    sections = lax.axis_size("section")
    section_index = lax.axis_index("section")
    w_first, w_second = in_one_piece((f_weight[0], g_weight[0]), "dp", 0, 1)
    gain_pair = gains[0]
    row_count = out_pair.shape[0]
    pair_width = out_pair.shape[1]
    channels = pair_width // 2
    blocks = 8
    block_rows = row_count // blocks
    tick_count = blocks + sections - 1
    is_last = section_index == sections - 1

    def tick(tick_index, loop_state):
        pair_in, grad_in = (loop_state[0], loop_state[1])
        buffers = loop_state[2:]
        block_index = tick_index - (sections - 1 - section_index)
        active = jnp.logical_and(block_index >= 0, block_index < blocks)
        row_start = jnp.clip(block_index, 0, blocks - 1) * block_rows
        pair_here = jnp.where(
            is_last, lax.dynamic_slice_in_dim(out_pair, row_start, block_rows, 0), pair_in
        )
        grad_here = jnp.where(
            is_last, lax.dynamic_slice_in_dim(out_grad, row_start, block_rows, 0), grad_in
        )

        def compute(held):
            pair_buf, grad_buf, first_norms, first_deltas, second_norms, second_deltas, gain_acc = (
                held
            )
            results = coupling_back(
                pair_here[:, :channels],
                pair_here[:, channels:],
                grad_here[:, :channels].astype(jnp.float32),
                grad_here[:, channels:].astype(jnp.float32),
                w_first,
                w_second,
                gain_pair,
            )
            new_pair = jnp.concatenate([results[0], results[1]], axis=1)
            new_grad = jnp.concatenate([results[2], results[3]], axis=1)
            return (
                lax.dynamic_update_slice_in_dim(pair_buf, new_pair, row_start, 0),
                lax.dynamic_update_slice_in_dim(grad_buf, new_grad, row_start, 0),
                lax.dynamic_update_slice_in_dim(first_norms, results[4], row_start, 0),
                lax.dynamic_update_slice_in_dim(first_deltas, results[5], row_start, 0),
                lax.dynamic_update_slice_in_dim(second_norms, results[6], row_start, 0),
                lax.dynamic_update_slice_in_dim(second_deltas, results[7], row_start, 0),
                gain_acc + results[8],
                new_pair,
                new_grad,
            )

        def unchanged(held):
            return held + (
                jnp.zeros((block_rows, pair_width), jnp.float32),
                jnp.zeros((block_rows, pair_width), jnp.bfloat16),
            )

        updated = lax.cond(active, compute, unchanged, buffers)
        joined = jnp.concatenate([updated[7], updated[8].astype(jnp.float32)], axis=1)
        arrived = from_behind(joined.astype(jnp.bfloat16), "section", -1).astype(joined.dtype)
        sent_pair = arrived[:, :pair_width]
        sent_grad = arrived[:, pair_width:].astype(jnp.bfloat16)
        return (sent_pair, sent_grad) + updated[:7]

    initial = (
        jnp.zeros((block_rows, pair_width), jnp.float32),
        jnp.zeros((block_rows, pair_width), jnp.bfloat16),
        jnp.zeros((row_count, pair_width), jnp.float32),
        jnp.zeros((row_count, pair_width), jnp.bfloat16),
        jnp.zeros((row_count, channels), jnp.bfloat16),
        jnp.zeros((row_count, channels), jnp.bfloat16),
        jnp.zeros((row_count, channels), jnp.bfloat16),
        jnp.zeros((row_count, channels), jnp.bfloat16),
        jnp.zeros((2, channels), jnp.float32),
    )
    final_state = lax.fori_loop(0, tick_count, tick, initial)
    pair_buf, grad_buf, first_norms, first_deltas, second_norms, second_deltas, gain_acc = (
        final_state[2:]
    )
    contract_rows = (((0,), (0,)), ((), ()))
    first_part = lax.dot_general(
        first_norms, first_deltas, contract_rows, preferred_element_type=jnp.float32
    )
    second_part = lax.dot_general(
        second_norms, second_deltas, contract_rows, preferred_element_type=jnp.float32
    )
    first_sum, second_sum = tuple(
        (
            part.astype(jnp.float32)
            for part in sent_together(
                (first_part.astype(jnp.bfloat16), second_part.astype(jnp.bfloat16)), "dp", 0, 1
            )
        )
    )
    gain_total = lax.psum(gain_acc, "dp")
    return (pair_buf[None], grad_buf[None], first_sum[None], second_sum[None], gain_total[None])


def solution(mesh):
    placed = (
        P("dp", None),
        P("dp", None),
        P("section", "dp", None),
        P("section", "dp", None),
        P("section", None, None),
    )
    return jax.shard_map(
        shards,
        mesh=mesh,
        in_specs=placed,
        out_specs=(
            P("section", "dp", None),
            P("section", "dp", None),
            P("section", "dp", None),
            P("section", "dp", None),
            P("section", None, None),
        ),
        check_vma=False,
    )
```

profile of v0, /device:TPU:2, one launch (start us, length us, event | category | flops | bytes accessed | tf_op | source)
XLA Modules:
  0.0 722.4 jit_solution(5279875102858007164)
XLA Ops:
  9.0 85.5 %all-gather.2.cloned.1.call-done = bf16[1024,2048]{1,0:T(8,128)(2,1)} async-done(((bf16[64,2048]{1,0:T(8,128)(2,1)}), bf16[1024,2048]{1,0:T(8,128)(2,1)}) %all-gather.2.cloned.1.call-update) | async-done | bytes 4194320 | tf_op jit(solution)/shard_map/all_gather | solution.py:12
  100.6 506.6 %while.32 = (s32[]{:T(128)}, f32[16,2048]{1,0:T(8,128)S(1)}, bf16[16,2048]{1,0:T(8,128)(2,1)S(1)}, f32[128,2048]{1,0:T(8,128)}, bf16[128,2048]{1,0:T(8,128)(2,1)...) while((s32[]{:T(128)}, f32[16,2048]{1,0:T(8,128)S(1)}, ...), condition=%wide.region_9.10_spmd.clone, body=%wide.region_0.9_spmd.clone.sunk | while | flops 136267888 | bytes 20988308 | solution.py:168
  106.5 6.9 collective-permute-start
  116.1 6.9 collective-permute-start
  127.0 6.8 collective-permute-start
  136.5 6.9 collective-permute-start
  146.1 6.9 collective-permute-start
  155.6 6.8 collective-permute-start
  165.1 6.8 collective-permute-start
  193.4 6.8 collective-permute-start
  313.3 71.5 %collective-permute-done = bf16[16,4096]{1,0:T(8,128)(2,1)S(1)} collective-permute-done((bf16[16,4096]{1,0:T(8,128)(2,1)S(1)}, bf16[16,4096]{1,0:T(8,128)(2,1)S(1)}, u32[]{:S(2)}, u32[]{:S(2)}) %collective-permute-start) | collective-permute-done | bytes 131104 | tf_op jit(solution)/shard_map/while/body/eval_jaxpr/ppermute | solution.py:19
  384.9 7.9 %conditional.3 = (f32[128,2048]{1,0:T(8,128)}, bf16[128,2048]{1,0:T(8,128)(2,1)}, bf16[128,1024]{1,0:T(8,128)(2,1)S(1)}, bf16[128,1024]{1,0:T(8,128)(2,1)S(1)}, ...) conditional(s32[]{:T(128)} %convert_element_type.155, ...), branch_computations={%region_1.1_spmd, %region_2.8_spmd.clone} | conditional | flops 135972976 | bytes 19873738 | solution.py:150
  394.7 7.4 %collective-permute-done = bf16[16,4096]{1,0:T(8,128)(2,1)S(1)} collective-permute-done((bf16[16,4096]{1,0:T(8,128)(2,1)S(1)}, bf16[16,4096]{1,0:T(8,128)(2,1)S(1)}, u32[]{:S(2)}, u32[]{:S(2)}) %collective-permute-start) | collective-permute-done | bytes 131104 | tf_op jit(solution)/shard_map/while/body/eval_jaxpr/ppermute | solution.py:19
  402.1 7.9 %conditional.3 = (f32[128,2048]{1,0:T(8,128)}, bf16[128,2048]{1,0:T(8,128)(2,1)}, bf16[128,1024]{1,0:T(8,128)(2,1)S(1)}, bf16[128,1024]{1,0:T(8,128)(2,1)S(1)}, ...) conditional(s32[]{:T(128)} %convert_element_type.155, ...), branch_computations={%region_1.1_spmd, %region_2.8_spmd.clone} | conditional | flops 135972976 | bytes 19873738 | solution.py:150
  411.9 7.4 %collective-permute-done = bf16[16,4096]{1,0:T(8,128)(2,1)S(1)} collective-permute-done((bf16[16,4096]{1,0:T(8,128)(2,1)S(1)}, bf16[16,4096]{1,0:T(8,128)(2,1)S(1)}, u32[]{:S(2)}, u32[]{:S(2)}) %collective-permute-start) | collective-permute-done | bytes 131104 | tf_op jit(solution)/shard_map/while/body/eval_jaxpr/ppermute | solution.py:19
  419.3 7.9 %conditional.3 = (f32[128,2048]{1,0:T(8,128)}, bf16[128,2048]{1,0:T(8,128)(2,1)}, bf16[128,1024]{1,0:T(8,128)(2,1)S(1)}, bf16[128,1024]{1,0:T(8,128)(2,1)S(1)}, ...) conditional(s32[]{:T(128)} %convert_element_type.155, ...), branch_computations={%region_1.1_spmd, %region_2.8_spmd.clone} | conditional | flops 135972976 | bytes 19873738 | solution.py:150
  429.2 7.5 %collective-permute-done = bf16[16,4096]{1,0:T(8,128)(2,1)S(1)} collective-permute-done((bf16[16,4096]{1,0:T(8,128)(2,1)S(1)}, bf16[16,4096]{1,0:T(8,128)(2,1)S(1)}, u32[]{:S(2)}, u32[]{:S(2)}) %collective-permute-start) | collective-permute-done | bytes 131104 | tf_op jit(solution)/shard_map/while/body/eval_jaxpr/ppermute | solution.py:19
  436.7 7.9 %conditional.3 = (f32[128,2048]{1,0:T(8,128)}, bf16[128,2048]{1,0:T(8,128)(2,1)}, bf16[128,1024]{1,0:T(8,128)(2,1)S(1)}, bf16[128,1024]{1,0:T(8,128)(2,1)S(1)}, ...) conditional(s32[]{:T(128)} %convert_element_type.155, ...), branch_computations={%region_1.1_spmd, %region_2.8_spmd.clone} | conditional | flops 135972976 | bytes 19873738 | solution.py:150
  446.5 7.4 %collective-permute-done = bf16[16,4096]{1,0:T(8,128)(2,1)S(1)} collective-permute-done((bf16[16,4096]{1,0:T(8,128)(2,1)S(1)}, bf16[16,4096]{1,0:T(8,128)(2,1)S(1)}, u32[]{:S(2)}, u32[]{:S(2)}) %collective-permute-start) | collective-permute-done | bytes 131104 | tf_op jit(solution)/shard_map/while/body/eval_jaxpr/ppermute | solution.py:19
  453.9 7.9 %conditional.3 = (f32[128,2048]{1,0:T(8,128)}, bf16[128,2048]{1,0:T(8,128)(2,1)}, bf16[128,1024]{1,0:T(8,128)(2,1)S(1)}, bf16[128,1024]{1,0:T(8,128)(2,1)S(1)}, ...) conditional(s32[]{:T(128)} %convert_element_type.155, ...), branch_computations={%region_1.1_spmd, %region_2.8_spmd.clone} | conditional | flops 135972976 | bytes 19873738 | solution.py:150
  463.7 7.4 %collective-permute-done = bf16[16,4096]{1,0:T(8,128)(2,1)S(1)} collective-permute-done((bf16[16,4096]{1,0:T(8,128)(2,1)S(1)}, bf16[16,4096]{1,0:T(8,128)(2,1)S(1)}, u32[]{:S(2)}, u32[]{:S(2)}) %collective-permute-start) | collective-permute-done | bytes 131104 | tf_op jit(solution)/shard_map/while/body/eval_jaxpr/ppermute | solution.py:19
  471.1 7.9 %conditional.3 = (f32[128,2048]{1,0:T(8,128)}, bf16[128,2048]{1,0:T(8,128)(2,1)}, bf16[128,1024]{1,0:T(8,128)(2,1)S(1)}, bf16[128,1024]{1,0:T(8,128)(2,1)S(1)}, ...) conditional(s32[]{:T(128)} %convert_element_type.155, ...), branch_computations={%region_1.1_spmd, %region_2.8_spmd.clone} | conditional | flops 135972976 | bytes 19873738 | solution.py:150
  481.0 7.4 %collective-permute-done = bf16[16,4096]{1,0:T(8,128)(2,1)S(1)} collective-permute-done((bf16[16,4096]{1,0:T(8,128)(2,1)S(1)}, bf16[16,4096]{1,0:T(8,128)(2,1)S(1)}, u32[]{:S(2)}, u32[]{:S(2)}) %collective-permute-start) | collective-permute-done | bytes 131104 | tf_op jit(solution)/shard_map/while/body/eval_jaxpr/ppermute | solution.py:19
  488.4 7.9 %conditional.3 = (f32[128,2048]{1,0:T(8,128)}, bf16[128,2048]{1,0:T(8,128)(2,1)}, bf16[128,1024]{1,0:T(8,128)(2,1)S(1)}, bf16[128,1024]{1,0:T(8,128)(2,1)S(1)}, ...) conditional(s32[]{:T(128)} %convert_element_type.155, ...), branch_computations={%region_1.1_spmd, %region_2.8_spmd.clone} | conditional | flops 135972976 | bytes 19873738 | solution.py:150
  498.2 11.7 %collective-permute-done = bf16[16,4096]{1,0:T(8,128)(2,1)S(1)} collective-permute-done((bf16[16,4096]{1,0:T(8,128)(2,1)S(1)}, bf16[16,4096]{1,0:T(8,128)(2,1)S(1)}, u32[]{:S(2)}, u32[]{:S(2)}) %collective-permute-start) | collective-permute-done | bytes 131104 | tf_op jit(solution)/shard_map/while/body/eval_jaxpr/ppermute | solution.py:19
  510.0 7.9 %conditional.3 = (f32[128,2048]{1,0:T(8,128)}, bf16[128,2048]{1,0:T(8,128)(2,1)}, bf16[128,1024]{1,0:T(8,128)(2,1)S(1)}, bf16[128,1024]{1,0:T(8,128)(2,1)S(1)}, ...) conditional(s32[]{:T(128)} %convert_element_type.155, ...), branch_computations={%region_1.1_spmd, %region_2.8_spmd.clone} | conditional | flops 135972976 | bytes 19873738 | solution.py:150
  523.7 14.6 %collective-permute-start = (bf16[16,4096]{1,0:T(8,128)(2,1)S(1)}, bf16[16,4096]{1,0:T(8,128)(2,1)S(1)}, u32[]{:S(2)}, u32[]{:S(2)}) collective-permute-start(bf16[16,4096]{1,0:T(8,128)(2,1)S(1)} %pad_maximum_fusion.7), channel_id=1, source_target_pairs={{16,0},{32,16},{48,32},{64,48},{80,64},{96,80},{112,96},{128,112},... | collective-permute-start | bytes 393224 | tf_op jit(solution)/shard_map/while/body/eval_jaxpr/ppermute | solution.py:19
  541.1 6.8 collective-permute-start
  550.6 6.8 collective-permute-start
  597.7 6.9 collective-permute-start
  617.6 33.1 %psum.7 = f32[1,2,1024]{2,1,0:T(2,128)} all-reduce(f32[1,2,1024]{2,1,0:T(2,128)S(1)} %bitcast.40), channel_id=1, replica_groups=mesh['section'=32,'dp'=16] {'dp'}, use_global_device_ids=true, to_apply=%region_11.12 | all-reduce | flops 2048 | bytes 16384 | tf_op jit(solution)/shard_map/psum | solution.py:187
  650.7 61.6 %reduce-scatter.4.cloned.1.call-done = bf16[64,2048]{1,0:T(8,128)(2,1)} async-done(((bf16[1024,2048]{1,0:T(8,128)(2,1)}), bf16[64,2048]{1,0:T(8,128)(2,1)}) %reduce-scatter.4.cloned.1.call-update) | async-done | bytes 262160
  (417 shorter events, 308.2 us)
Async XLA Ops:
  7.2 87.4 %all-gather.2.cloned.1.call-start = ((), (), s32[]{:S(2)}) async-start(), calls=%async_computation.1 | async-start | bytes 4456448 | tf_op jit(solution)/shard_map/all_gather | solution.py:12
  8.9 703.4 %reduce-scatter.4.cloned.1.call-start = ((), (), s32[]{:S(2)}) async-start(), calls=%async_computation.2 | async-start | bytes 4456448
  106.5 9.4 %collective-permute-start = (bf16[16,4096]{1,0:T(8,128)(2,1)S(1)}, bf16[16,4096]{1,0:T(8,128)(2,1)S(1)}, u32[]{:S(2)}, u32[]{:S(2)}) collective-permute-start(bf16[16,4096]{1,0:T(8,128)(2,1)S(1)} %pad_maximum_fusion.7), channel_id=1, source_target_pairs={{16,0},{32,16},{48,32},{64,48},{80,64},{96,80},{112,96},{128,112},... | collective-permute-start | bytes 393224 | tf_op jit(solution)/shard_map/while/body/eval_jaxpr/ppermute | solution.py:19
  116.1 10.8 %collective-permute-start = (bf16[16,4096]{1,0:T(8,128)(2,1)S(1)}, bf16[16,4096]{1,0:T(8,128)(2,1)S(1)}, u32[]{:S(2)}, u32[]{:S(2)}) collective-permute-start(bf16[16,4096]{1,0:T(8,128)(2,1)S(1)} %pad_maximum_fusion.7), channel_id=1, source_target_pairs={{16,0},{32,16},{48,32},{64,48},{80,64},{96,80},{112,96},{128,112},... | collective-permute-start | bytes 393224 | tf_op jit(solution)/shard_map/while/body/eval_jaxpr/ppermute | solution.py:19
  127.0 9.4 %collective-permute-start = (bf16[16,4096]{1,0:T(8,128)(2,1)S(1)}, bf16[16,4096]{1,0:T(8,128)(2,1)S(1)}, u32[]{:S(2)}, u32[]{:S(2)}) collective-permute-start(bf16[16,4096]{1,0:T(8,128)(2,1)S(1)} %pad_maximum_fusion.7), channel_id=1, source_target_pairs={{16,0},{32,16},{48,32},{64,48},{80,64},{96,80},{112,96},{128,112},... | collective-permute-start | bytes 393224 | tf_op jit(solution)/shard_map/while/body/eval_jaxpr/ppermute | solution.py:19
  136.5 9.4 %collective-permute-start = (bf16[16,4096]{1,0:T(8,128)(2,1)S(1)}, bf16[16,4096]{1,0:T(8,128)(2,1)S(1)}, u32[]{:S(2)}, u32[]{:S(2)}) collective-permute-start(bf16[16,4096]{1,0:T(8,128)(2,1)S(1)} %pad_maximum_fusion.7), channel_id=1, source_target_pairs={{16,0},{32,16},{48,32},{64,48},{80,64},{96,80},{112,96},{128,112},... | collective-permute-start | bytes 393224 | tf_op jit(solution)/shard_map/while/body/eval_jaxpr/ppermute | solution.py:19
  146.1 9.4 %collective-permute-start = (bf16[16,4096]{1,0:T(8,128)(2,1)S(1)}, bf16[16,4096]{1,0:T(8,128)(2,1)S(1)}, u32[]{:S(2)}, u32[]{:S(2)}) collective-permute-start(bf16[16,4096]{1,0:T(8,128)(2,1)S(1)} %pad_maximum_fusion.7), channel_id=1, source_target_pairs={{16,0},{32,16},{48,32},{64,48},{80,64},{96,80},{112,96},{128,112},... | collective-permute-start | bytes 393224 | tf_op jit(solution)/shard_map/while/body/eval_jaxpr/ppermute | solution.py:19
  155.6 9.3 %collective-permute-start = (bf16[16,4096]{1,0:T(8,128)(2,1)S(1)}, bf16[16,4096]{1,0:T(8,128)(2,1)S(1)}, u32[]{:S(2)}, u32[]{:S(2)}) collective-permute-start(bf16[16,4096]{1,0:T(8,128)(2,1)S(1)} %pad_maximum_fusion.7), channel_id=1, source_target_pairs={{16,0},{32,16},{48,32},{64,48},{80,64},{96,80},{112,96},{128,112},... | collective-permute-start | bytes 393224 | tf_op jit(solution)/shard_map/while/body/eval_jaxpr/ppermute | solution.py:19
  165.1 9.3 %collective-permute-start = (bf16[16,4096]{1,0:T(8,128)(2,1)S(1)}, bf16[16,4096]{1,0:T(8,128)(2,1)S(1)}, u32[]{:S(2)}, u32[]{:S(2)}) collective-permute-start(bf16[16,4096]{1,0:T(8,128)(2,1)S(1)} %pad_maximum_fusion.7), channel_id=1, source_target_pairs={{16,0},{32,16},{48,32},{64,48},{80,64},{96,80},{112,96},{128,112},... | collective-permute-start | bytes 393224 | tf_op jit(solution)/shard_map/while/body/eval_jaxpr/ppermute | solution.py:19
  174.5 9.3 %collective-permute-start = (bf16[16,4096]{1,0:T(8,128)(2,1)S(1)}, bf16[16,4096]{1,0:T(8,128)(2,1)S(1)}, u32[]{:S(2)}, u32[]{:S(2)}) collective-permute-start(bf16[16,4096]{1,0:T(8,128)(2,1)S(1)} %pad_maximum_fusion.7), channel_id=1, source_target_pairs={{16,0},{32,16},{48,32},{64,48},{80,64},{96,80},{112,96},{128,112},... | collective-permute-start | bytes 393224 | tf_op jit(solution)/shard_map/while/body/eval_jaxpr/ppermute | solution.py:19
  183.9 9.3 %collective-permute-start = (bf16[16,4096]{1,0:T(8,128)(2,1)S(1)}, bf16[16,4096]{1,0:T(8,128)(2,1)S(1)}, u32[]{:S(2)}, u32[]{:S(2)}) collective-permute-start(bf16[16,4096]{1,0:T(8,128)(2,1)S(1)} %pad_maximum_fusion.7), channel_id=1, source_target_pairs={{16,0},{32,16},{48,32},{64,48},{80,64},{96,80},{112,96},{128,112},... | collective-permute-start | bytes 393224 | tf_op jit(solution)/shard_map/while/body/eval_jaxpr/ppermute | solution.py:19
  193.4 9.3 %collective-permute-start = (bf16[16,4096]{1,0:T(8,128)(2,1)S(1)}, bf16[16,4096]{1,0:T(8,128)(2,1)S(1)}, u32[]{:S(2)}, u32[]{:S(2)}) collective-permute-start(bf16[16,4096]{1,0:T(8,128)(2,1)S(1)} %pad_maximum_fusion.7), channel_id=1, source_target_pairs={{16,0},{32,16},{48,32},{64,48},{80,64},{96,80},{112,96},{128,112},... | collective-permute-start | bytes 393224 | tf_op jit(solution)/shard_map/while/body/eval_jaxpr/ppermute | solution.py:19
  202.8 9.3 %collective-permute-start = (bf16[16,4096]{1,0:T(8,128)(2,1)S(1)}, bf16[16,4096]{1,0:T(8,128)(2,1)S(1)}, u32[]{:S(2)}, u32[]{:S(2)}) collective-permute-start(bf16[16,4096]{1,0:T(8,128)(2,1)S(1)} %pad_maximum_fusion.7), channel_id=1, source_target_pairs={{16,0},{32,16},{48,32},{64,48},{80,64},{96,80},{112,96},{128,112},... | collective-permute-start | bytes 393224 | tf_op jit(solution)/shard_map/while/body/eval_jaxpr/ppermute | solution.py:19
  212.2 9.3 %collective-permute-start = (bf16[16,4096]{1,0:T(8,128)(2,1)S(1)}, bf16[16,4096]{1,0:T(8,128)(2,1)S(1)}, u32[]{:S(2)}, u32[]{:S(2)}) collective-permute-start(bf16[16,4096]{1,0:T(8,128)(2,1)S(1)} %pad_maximum_fusion.7), channel_id=1, source_target_pairs={{16,0},{32,16},{48,32},{64,48},{80,64},{96,80},{112,96},{128,112},... | collective-permute-start | bytes 393224 | tf_op jit(solution)/shard_map/while/body/eval_jaxpr/ppermute | solution.py:19
  221.7 9.3 %collective-permute-start = (bf16[16,4096]{1,0:T(8,128)(2,1)S(1)}, bf16[16,4096]{1,0:T(8,128)(2,1)S(1)}, u32[]{:S(2)}, u32[]{:S(2)}) collective-permute-start(bf16[16,4096]{1,0:T(8,128)(2,1)S(1)} %pad_maximum_fusion.7), channel_id=1, source_target_pairs={{16,0},{32,16},{48,32},{64,48},{80,64},{96,80},{112,96},{128,112},... | collective-permute-start | bytes 393224 | tf_op jit(solution)/shard_map/while/body/eval_jaxpr/ppermute | solution.py:19
  231.1 9.3 %collective-permute-start = (bf16[16,4096]{1,0:T(8,128)(2,1)S(1)}, bf16[16,4096]{1,0:T(8,128)(2,1)S(1)}, u32[]{:S(2)}, u32[]{:S(2)}) collective-permute-start(bf16[16,4096]{1,0:T(8,128)(2,1)S(1)} %pad_maximum_fusion.7), channel_id=1, source_target_pairs={{16,0},{32,16},{48,32},{64,48},{80,64},{96,80},{112,96},{128,112},... | collective-permute-start | bytes 393224 | tf_op jit(solution)/shard_map/while/body/eval_jaxpr/ppermute | solution.py:19
  240.5 9.3 %collective-permute-start = (bf16[16,4096]{1,0:T(8,128)(2,1)S(1)}, bf16[16,4096]{1,0:T(8,128)(2,1)S(1)}, u32[]{:S(2)}, u32[]{:S(2)}) collective-permute-start(bf16[16,4096]{1,0:T(8,128)(2,1)S(1)} %pad_maximum_fusion.7), channel_id=1, source_target_pairs={{16,0},{32,16},{48,32},{64,48},{80,64},{96,80},{112,96},{128,112},... | collective-permute-start | bytes 393224 | tf_op jit(solution)/shard_map/while/body/eval_jaxpr/ppermute | solution.py:19
  250.0 9.3 %collective-permute-start = (bf16[16,4096]{1,0:T(8,128)(2,1)S(1)}, bf16[16,4096]{1,0:T(8,128)(2,1)S(1)}, u32[]{:S(2)}, u32[]{:S(2)}) collective-permute-start(bf16[16,4096]{1,0:T(8,128)(2,1)S(1)} %pad_maximum_fusion.7), channel_id=1, source_target_pairs={{16,0},{32,16},{48,32},{64,48},{80,64},{96,80},{112,96},{128,112},... | collective-permute-start | bytes 393224 | tf_op jit(solution)/shard_map/while/body/eval_jaxpr/ppermute | solution.py:19
  259.4 9.3 %collective-permute-start = (bf16[16,4096]{1,0:T(8,128)(2,1)S(1)}, bf16[16,4096]{1,0:T(8,128)(2,1)S(1)}, u32[]{:S(2)}, u32[]{:S(2)}) collective-permute-start(bf16[16,4096]{1,0:T(8,128)(2,1)S(1)} %pad_maximum_fusion.7), channel_id=1, source_target_pairs={{16,0},{32,16},{48,32},{64,48},{80,64},{96,80},{112,96},{128,112},... | collective-permute-start | bytes 393224 | tf_op jit(solution)/shard_map/while/body/eval_jaxpr/ppermute | solution.py:19
  268.8 9.3 %collective-permute-start = (bf16[16,4096]{1,0:T(8,128)(2,1)S(1)}, bf16[16,4096]{1,0:T(8,128)(2,1)S(1)}, u32[]{:S(2)}, u32[]{:S(2)}) collective-permute-start(bf16[16,4096]{1,0:T(8,128)(2,1)S(1)} %pad_maximum_fusion.7), channel_id=1, source_target_pairs={{16,0},{32,16},{48,32},{64,48},{80,64},{96,80},{112,96},{128,112},... | collective-permute-start | bytes 393224 | tf_op jit(solution)/shard_map/while/body/eval_jaxpr/ppermute | solution.py:19
  306.5 78.3 %collective-permute-start = (bf16[16,4096]{1,0:T(8,128)(2,1)S(1)}, bf16[16,4096]{1,0:T(8,128)(2,1)S(1)}, u32[]{:S(2)}, u32[]{:S(2)}) collective-permute-start(bf16[16,4096]{1,0:T(8,128)(2,1)S(1)} %pad_maximum_fusion.7), channel_id=1, source_target_pairs={{16,0},{32,16},{48,32},{64,48},{80,64},{96,80},{112,96},{128,112},... | collective-permute-start | bytes 393224 | tf_op jit(solution)/shard_map/while/body/eval_jaxpr/ppermute | solution.py:19
  427.2 9.4 %collective-permute-start = (bf16[16,4096]{1,0:T(8,128)(2,1)S(1)}, bf16[16,4096]{1,0:T(8,128)(2,1)S(1)}, u32[]{:S(2)}, u32[]{:S(2)}) collective-permute-start(bf16[16,4096]{1,0:T(8,128)(2,1)S(1)} %pad_maximum_fusion.7), channel_id=1, source_target_pairs={{16,0},{32,16},{48,32},{64,48},{80,64},{96,80},{112,96},{128,112},... | collective-permute-start | bytes 393224 | tf_op jit(solution)/shard_map/while/body/eval_jaxpr/ppermute | solution.py:19
  479.0 9.4 %collective-permute-start = (bf16[16,4096]{1,0:T(8,128)(2,1)S(1)}, bf16[16,4096]{1,0:T(8,128)(2,1)S(1)}, u32[]{:S(2)}, u32[]{:S(2)}) collective-permute-start(bf16[16,4096]{1,0:T(8,128)(2,1)S(1)} %pad_maximum_fusion.7), channel_id=1, source_target_pairs={{16,0},{32,16},{48,32},{64,48},{80,64},{96,80},{112,96},{128,112},... | collective-permute-start | bytes 393224 | tf_op jit(solution)/shard_map/while/body/eval_jaxpr/ppermute | solution.py:19
  496.3 13.6 %collective-permute-start = (bf16[16,4096]{1,0:T(8,128)(2,1)S(1)}, bf16[16,4096]{1,0:T(8,128)(2,1)S(1)}, u32[]{:S(2)}, u32[]{:S(2)}) collective-permute-start(bf16[16,4096]{1,0:T(8,128)(2,1)S(1)} %pad_maximum_fusion.7), channel_id=1, source_target_pairs={{16,0},{32,16},{48,32},{64,48},{80,64},{96,80},{112,96},{128,112},... | collective-permute-start | bytes 393224 | tf_op jit(solution)/shard_map/while/body/eval_jaxpr/ppermute | solution.py:19
  523.7 17.3 %collective-permute-start = (bf16[16,4096]{1,0:T(8,128)(2,1)S(1)}, bf16[16,4096]{1,0:T(8,128)(2,1)S(1)}, u32[]{:S(2)}, u32[]{:S(2)}) collective-permute-start(bf16[16,4096]{1,0:T(8,128)(2,1)S(1)} %pad_maximum_fusion.7), channel_id=1, source_target_pairs={{16,0},{32,16},{48,32},{64,48},{80,64},{96,80},{112,96},{128,112},... | collective-permute-start | bytes 393224 | tf_op jit(solution)/shard_map/while/body/eval_jaxpr/ppermute | solution.py:19
  541.1 9.3 %collective-permute-start = (bf16[16,4096]{1,0:T(8,128)(2,1)S(1)}, bf16[16,4096]{1,0:T(8,128)(2,1)S(1)}, u32[]{:S(2)}, u32[]{:S(2)}) collective-permute-start(bf16[16,4096]{1,0:T(8,128)(2,1)S(1)} %pad_maximum_fusion.7), channel_id=1, source_target_pairs={{16,0},{32,16},{48,32},{64,48},{80,64},{96,80},{112,96},{128,112},... | collective-permute-start | bytes 393224 | tf_op jit(solution)/shard_map/while/body/eval_jaxpr/ppermute | solution.py:19
  550.6 9.3 %collective-permute-start = (bf16[16,4096]{1,0:T(8,128)(2,1)S(1)}, bf16[16,4096]{1,0:T(8,128)(2,1)S(1)}, u32[]{:S(2)}, u32[]{:S(2)}) collective-permute-start(bf16[16,4096]{1,0:T(8,128)(2,1)S(1)} %pad_maximum_fusion.7), channel_id=1, source_target_pairs={{16,0},{32,16},{48,32},{64,48},{80,64},{96,80},{112,96},{128,112},... | collective-permute-start | bytes 393224 | tf_op jit(solution)/shard_map/while/body/eval_jaxpr/ppermute | solution.py:19
  560.0 9.3 %collective-permute-start = (bf16[16,4096]{1,0:T(8,128)(2,1)S(1)}, bf16[16,4096]{1,0:T(8,128)(2,1)S(1)}, u32[]{:S(2)}, u32[]{:S(2)}) collective-permute-start(bf16[16,4096]{1,0:T(8,128)(2,1)S(1)} %pad_maximum_fusion.7), channel_id=1, source_target_pairs={{16,0},{32,16},{48,32},{64,48},{80,64},{96,80},{112,96},{128,112},... | collective-permute-start | bytes 393224 | tf_op jit(solution)/shard_map/while/body/eval_jaxpr/ppermute | solution.py:19
  569.5 9.3 %collective-permute-start = (bf16[16,4096]{1,0:T(8,128)(2,1)S(1)}, bf16[16,4096]{1,0:T(8,128)(2,1)S(1)}, u32[]{:S(2)}, u32[]{:S(2)}) collective-permute-start(bf16[16,4096]{1,0:T(8,128)(2,1)S(1)} %pad_maximum_fusion.7), channel_id=1, source_target_pairs={{16,0},{32,16},{48,32},{64,48},{80,64},{96,80},{112,96},{128,112},... | collective-permute-start | bytes 393224 | tf_op jit(solution)/shard_map/while/body/eval_jaxpr/ppermute | solution.py:19
  578.9 9.3 %collective-permute-start = (bf16[16,4096]{1,0:T(8,128)(2,1)S(1)}, bf16[16,4096]{1,0:T(8,128)(2,1)S(1)}, u32[]{:S(2)}, u32[]{:S(2)}) collective-permute-start(bf16[16,4096]{1,0:T(8,128)(2,1)S(1)} %pad_maximum_fusion.7), channel_id=1, source_target_pairs={{16,0},{32,16},{48,32},{64,48},{80,64},{96,80},{112,96},{128,112},... | collective-permute-start | bytes 393224 | tf_op jit(solution)/shard_map/while/body/eval_jaxpr/ppermute | solution.py:19
  588.3 9.3 %collective-permute-start = (bf16[16,4096]{1,0:T(8,128)(2,1)S(1)}, bf16[16,4096]{1,0:T(8,128)(2,1)S(1)}, u32[]{:S(2)}, u32[]{:S(2)}) collective-permute-start(bf16[16,4096]{1,0:T(8,128)(2,1)S(1)} %pad_maximum_fusion.7), channel_id=1, source_target_pairs={{16,0},{32,16},{48,32},{64,48},{80,64},{96,80},{112,96},{128,112},... | collective-permute-start | bytes 393224 | tf_op jit(solution)/shard_map/while/body/eval_jaxpr/ppermute | solution.py:19
  597.7 9.4 %collective-permute-start = (bf16[16,4096]{1,0:T(8,128)(2,1)S(1)}, bf16[16,4096]{1,0:T(8,128)(2,1)S(1)}, u32[]{:S(2)}, u32[]{:S(2)}) collective-permute-start(bf16[16,4096]{1,0:T(8,128)(2,1)S(1)} %pad_maximum_fusion.7), channel_id=1, source_target_pairs={{16,0},{32,16},{48,32},{64,48},{80,64},{96,80},{112,96},{128,112},... | collective-permute-start | bytes 393224 | tf_op jit(solution)/shard_map/while/body/eval_jaxpr/ppermute | solution.py:19
  (18 other events, 100.6 us)
Sparse Core Ops, SparseCore 0:
  10.6 83.8 all-gather.1
  617.7 94.5 reduce-scatter.3
where the time goes:
time: 724 us; the launch traced here: 722 us
  waiting for transfers between devices  356 us (49%)
  starting transfers between devices  230 us (32%)
  matrix products  35.7 us (5%)
  blocking collectives  33.1 us (5%)
  other arithmetic  33 us (5%)
  local copies, waits for them, and re-layouts  16.3 us (2%)
  between operations  14.1 us (2%)
    ppermute x39, starting transfers between devices, from_behind(): return lax.ppermute(array, axis, pairs)  230 us
    ppermute x39, waiting for transfers between devices, from_behind(): return lax.ppermute(array, axis, pairs)  209 us
    all_gather x1, waiting for transfers between devices, in_one_piece(): result = lax.all_gather(both, axis, axis=dim, tiled=True)  85.5 us
    unnamed x3, waiting for transfers between devices  61.7 us
    psum x1, blocking collectives, shards(): gain_total = lax.psum(gain_acc, 'dp')  33.1 us
    dot_general x8, matrix products, coupling_back(): jnp.dot(normed_second, w_second, preferred_element_type=jnp.float32)  18.3 us
  transfers between devices with their start and end apart: 41, of which 41 were waited for; matrix products, arithmetic and copies ran while one was open for 0% of the time, Pallas kernels for 0%

commit v1 on v0

v1 whole, which is shorter than its diff:
```python
import functools

import jax
import jax.numpy as jnp
from jax import lax
from jax.experimental import pallas as pl
from jax.experimental.pallas import tpu as pltpu
from jax.sharding import PartitionSpec as P

MESH = pl.DeviceIdType.MESH
BF = jnp.bfloat16
F32 = jnp.float32
OFFSET = 0.25
NY = 2
ROWS = 16


def arrived(ref, sem):
    pltpu.make_async_copy(ref, ref, sem).wait()


def relay_kernel(
    n_section, n_dp, top_pair, top_grad, f_own, g_own, gains_own,
    pair_out, grad_out, part_out, gain_out,
    W, gain, ract, rgrad, nbuf, obuf, xbuf, rbuf, dbuf, gbuf, gacc, gsum,
    s_own, w_recv, w_peer, s_d2d, s_y, s_z, s_gain,
    s_ract, s_next, s_rgrad, s_gnext, s_x, r_x, s_r, r_r, s_pair, r_pair, s_d, r_d, s_grad, r_grad, s_gs,
):
    section = lax.axis_index("section")
    dp = lax.axis_index("dp")
    core = lax.rem(section, 2)
    chip = section // 2
    chips = n_section // 2
    nz = n_dp // NY
    half = nz // 2
    y, z = dp // nz, lax.rem(dp, nz)
    slab, dh = f_own.shape[1], f_own.shape[2]
    tok = ract.shape[0]
    blocks = tok // ROWS
    first = chip == chips - 1
    last = chip == 0
    partner = {"section": section + 1 - 2 * core}
    y_peer = {"dp": (1 - y) * nz + z}

    def z_peer(sign):
        return {"dp": y * nz + lax.rem(z + sign + nz, nz)}

    def remote(src, dst, send, recv, where):
        return pltpu.make_async_remote_copy(
            src_ref=src, dst_ref=dst, send_sem=send, recv_sem=recv, device_id=where, device_id_type=MESH
        )

    barrier = pltpu.get_barrier_semaphore()
    for where in (partner, y_peer, z_peer(1), z_peer(-1)):
        pl.semaphore_signal(barrier, inc=1, device_id=where, device_id_type=MESH)

    @pl.when(chip < chips - 1)
    def _():
        pl.semaphore_signal(barrier, inc=1, device_id={"section": section + 2}, device_id_type=MESH)

    @pl.when(chip > 0)
    def _():
        pl.semaphore_signal(barrier, inc=1, device_id={"section": section - 2}, device_id_type=MESH)

    own_f = pltpu.make_async_copy(f_own.at[0], W.at[core, 0, pl.ds(dp * slab, slab), :], s_own.at[0])
    own_g = pltpu.make_async_copy(g_own.at[0], W.at[core, 1, pl.ds(dp * slab, slab), :], s_own.at[1])
    own_c = pltpu.make_async_copy(gains_own.at[0], gain.at[core], s_own.at[2])
    own_g.start()
    own_f.start()
    own_c.start()
    gacc[...] = jnp.zeros_like(gacc)
    pl.semaphore_wait(barrier, 4 + jnp.where(chip < chips - 1, 1, 0) + jnp.where(chip > 0, 1, 0))

    def top_copy(b, part, src, dst, sem):
        rows, cols = pl.ds(b * ROWS, ROWS), pl.ds(part * dh, dh)
        return pltpu.make_async_copy(src.at[rows, cols], dst.at[rows, cols], sem.at[b, part])

    @pl.when(jnp.logical_and(first, core == 1))
    def _():
        def go(b, _):
            top_copy(b, 0, top_pair, ract, s_ract).start()
            top_copy(b, 1, top_pair, ract, s_ract).start()
            return 0
        lax.fori_loop(0, blocks, go, 0)

    @pl.when(jnp.logical_and(first, core == 0))
    def _():
        def go(b, _):
            top_copy(b, 0, top_grad, rgrad, s_rgrad).start()
            top_copy(b, 1, top_grad, rgrad, s_rgrad).start()
            return 0
        lax.fori_loop(0, blocks, go, 0)

    def index_of(plane, zz):
        return plane * nz + lax.rem(zz + nz, nz)

    def item(h, index):
        return W.at[core, h, pl.ds(index * slab, slab), :]

    def to_peer(h, index):
        return remote(item(h, index), item(h, index), s_d2d.at[h, index], w_peer.at[h, index], partner)

    def to_y(h, index):
        return remote(item(h, index), item(h, index), s_y.at[h, index], w_recv.at[h, index], y_peer)

    CHAINS = ((1, 0), (1, 1), (0, 0))

    def to_z(chain, direction, step, sign):
        h, other = CHAINS[chain]
        plane = y if other == 0 else 1 - y
        index = index_of(plane, z - sign * step)
        return remote(item(h, index), item(h, index), s_z.at[chain, direction, step], w_recv.at[h, index], z_peer(sign))

    long_sign = 1 - 2 * core

    def sends(chain, step):
        if step < half - 1:
            return [to_z(chain, 0, step, 1), to_z(chain, 1, step, -1)]
        return [to_z(chain, 0, step, long_sign)]

    own_g.wait()
    to_y(1, dp).start()
    for copy in sends(0, 0):
        copy.start()
    own_f.wait()
    for copy in sends(2, 0):
        copy.start()
    to_y(0, dp).start()
    to_peer(1, dp).start()
    to_peer(0, dp).start()
    own_c.wait()
    gain_copy = remote(gain.at[core], gain.at[core], s_gain.at[0], s_gain.at[1], partner)
    gain_copy.start()
    other_own = index_of(1 - y, z)
    arrived(item(1, other_own), w_recv.at[1, other_own])
    for copy in sends(1, 0):
        copy.start()
    to_peer(1, other_own).start()
    for step in range(1, half + 1):
        for chain in (0, 1, 2):
            h, other = CHAINS[chain]
            plane = y if other == 0 else 1 - y
            for sign in (1, -1) if step < half else (1,):
                index = index_of(plane, z - sign * step)
                arrived(item(h, index), w_recv.at[h, index])
                if step < half - 1:
                    to_z(chain, 0 if sign == 1 else 1, step, sign).start()
                to_peer(h, index).start()
                if h == 0:
                    to_y(0, index).start()
            if step == half - 1:
                for copy in sends(chain, step):
                    copy.start()
    for zz in range(nz):
        index = index_of(1 - y, z + zz)
        arrived(item(0, index), w_recv.at[0, index])
        to_peer(0, index).start()

    def peer_item(h, index):
        return W.at[1 - core, h, pl.ds(index * slab, slab), :]

    def peer_wait(index, _):
        for h in (1, 0):
            arrived(peer_item(h, index), w_peer.at[h, index])
        return 0

    lax.fori_loop(0, n_dp, peer_wait, 0)
    arrived(gain.at[1 - core], s_gain.at[1])

    def rows_of(b):
        return pl.ds(pl.multiple_of(b * ROWS, ROWS), ROWS)

    def next_copy(b, part):
        rows, cols = rows_of(b), pl.ds(part * dh, dh)
        return remote(nbuf.at[rows, cols], ract.at[rows, cols], s_next.at[b, part], s_ract.at[b, part], {"section": section - 2})

    def gnext_copy(b, part):
        rows, cols = rows_of(b), pl.ds(part * dh, dh)
        return remote(gbuf.at[0, rows, cols], rgrad.at[rows, cols], s_gnext.at[b, part], s_rgrad.at[b, part], {"section": section - 2})

    def x_copy(lay, b):
        at = xbuf.at[lay, :, rows_of(b), :]
        return remote(at, at, s_x.at[lay, b], r_x.at[lay, b], partner)

    def r_copy(lay, b):
        at = rbuf.at[lay, :, rows_of(b), :]
        return remote(at, at, s_r.at[lay, b], r_r.at[lay, b], partner)

    def d_copy(b):
        at = dbuf.at[1, :, rows_of(b), :]
        return remote(at, at, s_d.at[b], r_d.at[b], partner)

    def pair_copy(lay, b):
        src, dst = obuf.at[lay, rows_of(b), :], pair_out.at[0, rows_of(b), :]
        if lay == 1:
            return pltpu.make_async_copy(src, dst, s_pair.at[lay, b])
        return remote(src, dst, s_pair.at[lay, b], r_pair.at[b], partner)

    def grad_copy(lay, b):
        src, dst = gbuf.at[lay, rows_of(b), :], grad_out.at[0, rows_of(b), :]
        if lay == 0:
            return pltpu.make_async_copy(src, dst, s_grad.at[lay, b])
        return remote(src, dst, s_grad.at[lay, b], r_grad.at[b], partner)

    def sent(copy, is_local):
        if is_local:
            copy.wait()
        else:
            copy.wait_send()

    @pl.when(core == 1)
    def _():
        def act(b, _):
            rows = rows_of(b)
            for part in (1, 0):
                cols = pl.ds(part * dh, dh)
                arrived(ract.at[rows, cols], s_ract.at[b, part])
            y1 = ract[rows, :dh].astype(F32)
            y2 = ract[rows, dh:].astype(F32)
            for lay in (1, 0):
                cf, cg = gain[lay, 0:1, :], gain[lay, 1:2, :]
                rg = lax.rsqrt(jnp.mean(y1 * y1, axis=-1, keepdims=True) + OFFSET)
                ug = y1 * rg
                pre = jnp.dot((ug * cg).astype(BF), W[lay, 1], preferred_element_type=F32)
                sig = jax.nn.sigmoid(pre)
                silu = pre * sig
                x2 = y2 - silu
                sg = sig + silu * (1.0 - sig)
                obuf[lay, rows, dh:] = x2
                if lay == 0:
                    nbuf[rows, dh:] = x2.astype(BF)

                    @pl.when(jnp.logical_not(last))
                    def _():
                        next_copy(b, 1).start()
                rf = lax.rsqrt(jnp.mean(x2 * x2, axis=-1, keepdims=True) + OFFSET)
                uf = x2 * rf
                pre = jnp.dot((uf * cf).astype(BF), W[lay, 0], preferred_element_type=F32)
                sig = jax.nn.sigmoid(pre)
                silu = pre * sig
                x1 = y1 - silu
                sf = sig + silu * (1.0 - sig)
                if lay == 0:
                    nbuf[rows, :dh] = x1.astype(BF)

                    @pl.when(jnp.logical_not(last))
                    def _():
                        next_copy(b, 0).start()
                obuf[lay, rows, :dh] = x1
                xbuf[lay, 0, rows, :] = uf.astype(BF)
                xbuf[lay, 1, rows, :] = ug.astype(BF)
                xbuf[lay, 2, rows, :] = sf.astype(BF)
                xbuf[lay, 3, rows, :] = sg.astype(BF)
                rbuf[lay, 0, rows, :] = jnp.broadcast_to(rf, (ROWS, 128))
                rbuf[lay, 1, rows, :] = jnp.broadcast_to(rg, (ROWS, 128))
                x_copy(lay, b).start()
                r_copy(lay, b).start()
                pair_copy(lay, b).start()
                y1, y2 = x1, x2
            return 0

        lax.fori_loop(0, blocks, act, 0)

    def times_transposed(delta, weight):
        return lax.dot_general(delta, weight, (((1,), (1,)), ((), ())), preferred_element_type=F32)

    @pl.when(core == 0)
    def _():
        def grad(b, _):
            rows = rows_of(b)
            for part in (0, 1):
                cols = pl.ds(part * dh, dh)
                arrived(rgrad.at[rows, cols], s_rgrad.at[b, part])
            gy1 = rgrad[rows, :dh].astype(F32)
            gy2 = rgrad[rows, dh:].astype(F32)
            for lay in (1, 0):
                arrived(xbuf.at[lay, :, rows, :], r_x.at[lay, b])
                arrived(rbuf.at[lay, :, rows, :], r_r.at[lay, b])
                cf, cg = gain[lay, 0:1, :], gain[lay, 1:2, :]
                uf, ug = xbuf[lay, 0, rows, :].astype(F32), xbuf[lay, 1, rows, :].astype(F32)
                sf, sg = xbuf[lay, 2, rows, :].astype(F32), xbuf[lay, 3, rows, :].astype(F32)
                rf, rg = rbuf[lay, 0, rows, 0:1], rbuf[lay, 1, rows, 0:1]
                delta = (gy2 * sg).astype(BF)
                dbuf[lay, 1, rows, :] = delta
                back = times_transposed(delta, W[lay, 1])
                gacc[lay, 1] += back * ug
                w = cg * back
                gz = gy1 + rg * (w - ug * jnp.mean(w * ug, axis=-1, keepdims=True))
                gbuf[lay, rows, :dh] = gz.astype(BF)
                if lay == 0:
                    @pl.when(jnp.logical_not(last))
                    def _():
                        gnext_copy(b, 0).start()
                delta = (gz * sf).astype(BF)
                dbuf[lay, 0, rows, :] = delta
                back = times_transposed(delta, W[lay, 0])
                gacc[lay, 0] += back * uf
                w = cf * back
                gx = gy2 + rf * (w - uf * jnp.mean(w * uf, axis=-1, keepdims=True))
                gbuf[lay, rows, dh:] = gx.astype(BF)
                if lay == 0:
                    @pl.when(jnp.logical_not(last))
                    def _():
                        gnext_copy(b, 1).start()
                else:
                    d_copy(b).start()
                grad_copy(lay, b).start()
                gy1, gy2 = gz, gx
            return 0

        lax.fori_loop(0, blocks, grad, 0)
        for lay in (0, 1):
            gsum[lay] = jnp.sum(gacc[lay], axis=1)
        remote(gsum.at[1], gsum.at[1], s_gs.at[0], s_gs.at[1], partner).start()

    @pl.when(core == 1)
    def _():
        def wait_d(b, _):
            arrived(dbuf.at[1, :, rows_of(b), :], r_d.at[b])
            return 0
        lax.fori_loop(0, blocks, wait_d, 0)
        arrived(gsum.at[1], s_gs.at[1])

    gain_out[0] = gsum[core]
    width = min(128, dh)

    def outer(i, _):
        at = pl.ds(pl.multiple_of(i * width, width), width)
        for h in (0, 1):
            normed = (xbuf[core, h, :, at].astype(F32) * gain[core, h, at][None, :]).astype(BF)
            part = lax.dot_general(normed, dbuf[core, h], (((0,), (0,)), ((), ())), preferred_element_type=F32)
            part_out[at, h * dh:(h + 1) * dh] = part.astype(BF)
        return 0

    lax.fori_loop(0, dh // width, outer, 0)

    @pl.when(core == 1)
    def _():
        def done(b, _):
            for lay in (0, 1):
                x_copy(lay, b).wait_send()
                r_copy(lay, b).wait_send()
                sent(pair_copy(lay, b), lay == 1)
            arrived(grad_out.at[0, rows_of(b), :], r_grad.at[b])

            @pl.when(jnp.logical_not(last))
            def _():
                next_copy(b, 0).wait_send()
                next_copy(b, 1).wait_send()
            return 0
        lax.fori_loop(0, blocks, done, 0)

    @pl.when(core == 0)
    def _():
        def done(b, _):
            d_copy(b).wait_send()
            for lay in (0, 1):
                sent(grad_copy(lay, b), lay == 0)
            arrived(pair_out.at[0, rows_of(b), :], r_pair.at[b])

            @pl.when(jnp.logical_not(last))
            def _():
                gnext_copy(b, 0).wait_send()
                gnext_copy(b, 1).wait_send()
            return 0
        lax.fori_loop(0, blocks, done, 0)
        remote(gsum.at[1], gsum.at[1], s_gs.at[0], s_gs.at[1], partner).wait_send()

    gain_copy.wait_send()
    to_y(1, dp).wait_send()

    def y_done(zz, _):
        to_y(0, index_of(y, zz)).wait_send()
        return 0
    lax.fori_loop(0, nz, y_done, 0)

    def peer_done(index, _):
        to_peer(0, index).wait_send()
        to_peer(1, index).wait_send()
        return 0
    lax.fori_loop(0, n_dp, peer_done, 0)
    for chain in (0, 1, 2):
        for step in range(half):
            for copy in sends(chain, step):
                copy.wait_send()


def shards(n_section, n_dp, out_pair, out_grad, f_weight, g_weight, gains):
    tok, width = out_pair.shape
    dh = width // 2
    slab = f_weight.shape[1]
    blocks = tok // ROWS
    nz = n_dp // NY
    half = nz // 2
    any_space = pl.BlockSpec(memory_space=pl.ANY)
    vmem = pl.BlockSpec(memory_space=pltpu.VMEM)
    dma = pltpu.SemaphoreType.DMA
    pair, grad, part, gain = pl.pallas_call(
        functools.partial(relay_kernel, n_section, n_dp),
        out_shape=(
            jax.ShapeDtypeStruct((1, tok, width), F32),
            jax.ShapeDtypeStruct((1, tok, width), BF),
            jax.ShapeDtypeStruct((dh, width), BF),
            jax.ShapeDtypeStruct((1, 2, dh), F32),
        ),
        in_specs=[any_space] * 5,
        out_specs=(any_space, any_space, vmem, vmem),
        scratch_shapes=[
            pltpu.VMEM((2, 2, dh, dh), BF),
            pltpu.VMEM((2, 2, dh), F32),
            pltpu.VMEM((tok, width), BF),
            pltpu.VMEM((tok, width), BF),
            pltpu.VMEM((tok, width), BF),
            pltpu.VMEM((2, tok, width), F32),
            pltpu.VMEM((2, 4, tok, dh), BF),
            pltpu.VMEM((2, 2, tok, 128), F32),
            pltpu.VMEM((2, 2, tok, dh), BF),
            pltpu.VMEM((2, tok, width), BF),
            pltpu.VMEM((2, 2, ROWS, dh), F32),
            pltpu.VMEM((2, 2, dh), F32),
            dma((3,)), dma((2, n_dp)), dma((2, n_dp)), dma((2, n_dp)), dma((2, n_dp)), dma((3, 2, half)), dma((2,)),
            dma((blocks, 2)), dma((blocks, 2)), dma((blocks, 2)), dma((blocks, 2)),
            dma((2, blocks)), dma((2, blocks)), dma((2, blocks)), dma((2, blocks)),
            dma((2, blocks)), dma((blocks,)), dma((blocks,)), dma((blocks,)), dma((2, blocks)), dma((blocks,)), dma((2,)),
        ],
        compiler_params=pltpu.CompilerParams(
            collective_id=0, has_side_effects=True, vmem_limit_bytes=60 * 1024 * 1024
        ),
        name="relay",
    )(out_pair.astype(BF), out_grad, f_weight, g_weight, gains)
    summed = lax.psum_scatter(part, "dp", scatter_dimension=0, tiled=True).astype(F32)
    gain = lax.psum(gain, "dp")
    return pair, grad, summed[None, :, :dh], summed[None, :, dh:], gain


def solution(mesh):
    sizes = dict(mesh.shape)
    return jax.shard_map(
        functools.partial(shards, sizes["section"], sizes["dp"]),
        mesh=mesh,
        in_specs=(P("dp", None), P("dp", None), P("section", "dp", None), P("section", "dp", None), P("section", None, None)),
        out_specs=(
            P("section", "dp", None),
            P("section", "dp", None),
            P("section", "dp", None),
            P("section", "dp", None),
            P("section", None, None),
        ),
        check_vma=False,
    )
```

time: 724 us -> 294 us (0.41)
  the two profiles are of different devices: /device:TPU:2 before, /device:TPU:16 now
where the time goes in v1:
time: 294 us
  Pallas kernels  190 us (65%)
  waiting for transfers between devices  51.3 us (17%)
  blocking collectives  31.8 us (11%)
  between operations  14.1 us (5%)
  local copies, waits for them, and re-layouts  3.24 us (1%)
  other arithmetic  3.07 us (1%)
    pallas_call x1, Pallas kernels, shards(): pl.pallas_call(functools.partial(relay_kernel, n_section, n_dp), out_shap...  190 us
    reduce_scatter x1, waiting for transfers between devices, shards(): lax.psum_scatter(part, 'dp', scatter_dimension=0, tiled=True).astype(F32)  51.2 us
    psum x1, blocking collectives, shards(): gain = lax.psum(gain, 'dp')  31.8 us
  transfers between devices with their start and end apart: 1, of which 1 were waited for; matrix products, arithmetic and copies ran while one was open for 0% of the time, Pallas kernels for 0%

profile of v1, /device:TPU:16, one launch (start us, length us, event | category | flops | bytes accessed | tf_op | source)
XLA Modules:
  0.0 293.7 jit_solution(12197164270358793918)
XLA Ops:
  7.2 0.0 reduce-scatter.2.cloned.1.call-start
  7.2 2.1 convert_element_type.6.top_pair
  9.3 190.2 %relay.1 = (f32[1,128,2048]{2,1,0:T(8,128)}, bf16[1,128,2048]{2,1,0:T(8,128)(2,1)}, bf16[1024,2048]{1,0:T(8,128)(2,1)}, f32[1,2,1024]{2,1,0:T(2,128)}) custom-call(bf16[128,2048]{1,0:T(8,128)(2,1)} %convert_element_type.6.top_pair, bf16[128,2048]{1,0:T(8,128)(2,1)} %top_grad.1, bf16[1,64,1024]{2,1,0:T(8,128)(2,1)} %f_own.1, bf16[1,64,1024]{2,1,0:T(8,128)(2,1)} %g_own.1, ...), custom_call_target="tpu_custom_call" | custom-call | tf_op jit(solution)/shard_map/relay/pallas_call | solution.py:398
  199.5 0.0 copy-start.2
  199.5 0.0 copy-start
  199.6 0.0 copy-start.1
  199.6 0.0 reduce-scatter.2.cloned.1.call-update
  199.6 0.6 copy-done.2
  200.2 31.8 %psum.7 = f32[1,2,1024]{2,1,0:T(2,128)} all-reduce(f32[1,2,1024]{2,1,0:T(2,128)S(1)} %copy-done.2), channel_id=1, replica_groups=mesh['section'=32,'dp'=16] {'dp'}, use_global_device_ids=true, to_apply=%region_1.0 | all-reduce | flops 2048 | bytes 16384 | tf_op jit(solution)/shard_map/psum | solution.py:432
  232.0 51.2 %reduce-scatter.2.cloned.1.call-done = bf16[64,2048]{1,0:T(8,128)(2,1)} async-done(((bf16[1024,2048]{1,0:T(8,128)(2,1)}), bf16[64,2048]{1,0:T(8,128)(2,1)}) %reduce-scatter.2.cloned.1.call-update) | async-done | bytes 262160 | tf_op jit(solution)/shard_map/reduce_scatter | solution.py:431
  283.2 1.0 convert_element_type.7
  284.2 0.8 slice_bitcast_fusion
  285.1 0.0 copy-done
  285.1 1.0 copy.12
  286.0 0.0 copy-done.1
  286.0 0.8 copy.13
Async XLA Ops:
  7.2 276.1 %reduce-scatter.2.cloned.1.call-start = ((), (), s32[]{:S(2)}) async-start(), calls=%async_computation.1 | async-start | bytes 4456448 | tf_op jit(solution)/shard_map/reduce_scatter | solution.py:431
  199.5 0.7 copy-start.2
  199.5 85.5 %copy-start = (f32[1,128,2048]{2,1,0:T(8,128)S(1)}, f32[1,128,2048]{2,1,0:T(8,128)}, u32[]{:S(2)}) copy-start(f32[1,128,2048]{2,1,0:T(8,128)} %get-tuple-element.20) | copy-start | bytes 3145732
  199.6 86.5 %copy-start.1 = (bf16[1,128,2048]{2,1,0:T(8,128)(2,1)S(1)}, bf16[1,128,2048]{2,1,0:T(8,128)(2,1)}, u32[]{:S(2)}) copy-start(bf16[1,128,2048]{2,1,0:T(8,128)(2,1)} %get-tuple-element.21) | copy-start | bytes 1572868
Sparse Core Ops, SparseCore 0:
  199.7 83.4 reduce-scatter.1

commit v2 on v1

--- a/solution.py
+++ b/solution.py
@@ -21,10 +21,12 @@
 
 def relay_kernel(
     n_section, n_dp, top_pair, top_grad, f_own, g_own, gains_own,
-    pair_out, grad_out, part_out, gain_out,
+    pair_out, grad_out, f_out, g_out, gain_out,
     W, gain, ract, rgrad, nbuf, obuf, xbuf, rbuf, dbuf, gbuf, gacc, gsum,
+    P_, RZ, RY, YG, gslot, gmine, gpeer,
     s_own, w_recv, w_peer, s_d2d, s_y, s_z, s_gain,
     s_ract, s_next, s_rgrad, s_gnext, s_x, r_x, s_r, r_r, s_pair, r_pair, s_d, r_d, s_grad, r_grad, s_gs,
+    qs_z, qr_z, qs_y, qr_y, es_z, er_z, es_y,
 ):
     section = lax.axis_index("section")
     dp = lax.axis_index("dp")
@@ -77,11 +79,10 @@
 
     @pl.when(jnp.logical_and(first, core == 1))
     def _():
-        def go(b, _):
-            top_copy(b, 0, top_pair, ract, s_ract).start()
-            top_copy(b, 1, top_pair, ract, s_ract).start()
-            return 0
-        lax.fori_loop(0, blocks, go, 0)
+        load = pltpu.make_async_copy(top_pair, obuf.at[0], s_own.at[3])
+        load.start()
+        load.wait()
+        ract[...] = obuf[0].astype(BF)
 
     @pl.when(jnp.logical_and(first, core == 0))
     def _():
@@ -212,9 +213,13 @@
     def _():
         def act(b, _):
             rows = rows_of(b)
-            for part in (1, 0):
-                cols = pl.ds(part * dh, dh)
-                arrived(ract.at[rows, cols], s_ract.at[b, part])
+
+            @pl.when(jnp.logical_not(first))
+            def _():
+                for part in (1, 0):
+                    cols = pl.ds(part * dh, dh)
+                    arrived(ract.at[rows, cols], s_ract.at[b, part])
+
             y1 = ract[rows, :dh].astype(F32)
             y2 = ract[rows, dh:].astype(F32)
             for lay in (1, 0):
@@ -321,18 +326,112 @@
         lax.fori_loop(0, blocks, wait_d, 0)
         arrived(gsum.at[1], s_gs.at[1])
 
-    gain_out[0] = gsum[core]
+    gmine[...] = gsum[core]
+    e_y = remote(gmine, gpeer, es_y.at[0], es_y.at[1], y_peer)
+    e_y.start()
+
     width = min(128, dh)
 
-    def outer(i, _):
-        at = pl.ds(pl.multiple_of(i * width, width), width)
-        for h in (0, 1):
+    def weight_grad(h):
+        def outer(i, _):
+            at = pl.ds(pl.multiple_of(i * width, width), width)
             normed = (xbuf[core, h, :, at].astype(F32) * gain[core, h, at][None, :]).astype(BF)
-            part = lax.dot_general(normed, dbuf[core, h], (((0,), (0,)), ((), ())), preferred_element_type=F32)
-            part_out[at, h * dh:(h + 1) * dh] = part.astype(BF)
-        return 0
-
-    lax.fori_loop(0, dh // width, outer, 0)
+            P_[h, at, :] = lax.dot_general(
+                normed, dbuf[core, h], (((0,), (0,)), ((), ())), preferred_element_type=F32
+            ).astype(BF)
+            return 0
+
+        lax.fori_loop(0, dh // width, outer, 0)
+
+    signs, hops = (long_sign, -long_sign), (half, half - 1)
+    order = [(d, hops[d] - i) for i in range(half) for d in (0, 1) if i < hops[d]] + [(0, 0)]
+
+    def mine(h, plane, zz):
+        return P_.at[h, pl.ds(pl.multiple_of(index_of(plane, zz) * slab, slab), slab), :]
+
+    def f_to_y(zz):
+        zz = lax.rem(zz + nz, nz)
+        return remote(mine(0, 1 - y, zz), RY.at[zz], qs_y.at[zz], qr_y.at[zz], y_peer)
+
+    def ring(chain, d, i, source):
+        return remote(source, RZ.at[chain, d, i], qs_z.at[chain, d, i], qr_z.at[chain, d, i], z_peer(signs[d]))
+
+    def gains_ring(d, i):
+        at = gslot.at[lax.rem(z - signs[d] * i + nz, nz)]
+        return remote(at, at, es_z.at[d, i], er_z.at[d, i], z_peer(signs[d]))
+
+    weight_grad(0)
+    for d, far in order:
+        f_to_y(z + signs[d] * far).start()
+    weight_grad(1)
+    e_y.wait()
+    gslot[z] = gmine[...] + gpeer[...]
+
+    def terms(chain, zz):
+        h, other = ((1, 0), (1, 1), (0, 0))[chain]
+        own = mine(h, y if other == 0 else 1 - y, zz)
+        total = own[...].astype(F32)
+        if chain == 2:
+            zz = lax.rem(zz + nz, nz)
+            arrived(RY.at[zz], qr_y.at[zz])
+            total = total + RY[zz].astype(F32)
+        return own, total
+
+    for i in range(half):
+        for d in (0, 1):
+            if i < hops[d]:
+                if i > 0:
+                    arrived(gslot.at[lax.rem(z - signs[d] * i + nz, nz)], er_z.at[d, i - 1])
+                gains_ring(d, i).start()
+        for chain in (1, 0, 2):
+            for d in (0, 1):
+                if i >= hops[d]:
+                    continue
+                far = z + signs[d] * (hops[d] - i)
+                if i > 0:
+                    arrived(RZ.at[chain, d, i - 1], qr_z.at[chain, d, i - 1])
+                own, total = terms(chain, far)
+                if i > 0:
+                    source = RZ.at[chain, d, i - 1]
+                    source[...] = (total + source[...].astype(F32)).astype(BF)
+                else:
+                    source = own
+                    if chain == 2:
+                        source[...] = total.astype(BF)
+                ring(chain, d, i, source).start()
+
+    def total_of(chain):
+        for d in (0, 1):
+            if hops[d] > 0:
+                arrived(RZ.at[chain, d, hops[d] - 1], qr_z.at[chain, d, hops[d] - 1])
+        _, total = terms(chain, z)
+        for d in (0, 1):
+            if hops[d] > 0:
+                total = total + RZ[chain, d, hops[d] - 1].astype(F32)
+        return total
+
+    YG[...] = total_of(1).astype(BF)
+    g_to_y = remote(YG, RY.at[nz], qs_y.at[nz], qr_y.at[nz], y_peer)
+    g_to_y.start()
+    g_out[0] = total_of(0)
+    f_out[0] = total_of(2)
+    for d in (0, 1):
+        if hops[d] > 0:
+            arrived(gslot.at[lax.rem(z - signs[d] * hops[d] + nz, nz)], er_z.at[d, hops[d] - 1])
+    gain_total = gslot[0]
+    for zz in range(1, nz):
+        gain_total = gain_total + gslot[zz]
+    gain_out[0] = gain_total
+    arrived(RY.at[nz], qr_y.at[nz])
+    g_out[0] = g_out[0] + RY[nz].astype(F32)
+    g_to_y.wait_send()
+    for zz in range(nz):
+        f_to_y(z + zz).wait_send()
+    for d in (0, 1):
+        for i in range(hops[d]):
+            gains_ring(d, i).wait_send()
+            for chain in (0, 1, 2):
+                ring(chain, d, i, RZ.at[chain, d, i]).wait_send()
 
     @pl.when(core == 1)
     def _():
@@ -395,16 +494,17 @@
     any_space = pl.BlockSpec(memory_space=pl.ANY)
     vmem = pl.BlockSpec(memory_space=pltpu.VMEM)
     dma = pltpu.SemaphoreType.DMA
-    pair, grad, part, gain = pl.pallas_call(
+    return pl.pallas_call(
         functools.partial(relay_kernel, n_section, n_dp),
         out_shape=(
             jax.ShapeDtypeStruct((1, tok, width), F32),
             jax.ShapeDtypeStruct((1, tok, width), BF),
-            jax.ShapeDtypeStruct((dh, width), BF),
+            jax.ShapeDtypeStruct((1, slab, dh), F32),
+            jax.ShapeDtypeStruct((1, slab, dh), F32),
             jax.ShapeDtypeStruct((1, 2, dh), F32),
         ),
         in_specs=[any_space] * 5,
-        out_specs=(any_space, any_space, vmem, vmem),
+        out_specs=(any_space, any_space, vmem, vmem, vmem),
         scratch_shapes=[
             pltpu.VMEM((2, 2, dh, dh), BF),
             pltpu.VMEM((2, 2, dh), F32),
@@ -418,19 +518,24 @@
             pltpu.VMEM((2, tok, width), BF),
             pltpu.VMEM((2, 2, ROWS, dh), F32),
             pltpu.VMEM((2, 2, dh), F32),
-            dma((3,)), dma((2, n_dp)), dma((2, n_dp)), dma((2, n_dp)), dma((2, n_dp)), dma((3, 2, half)), dma((2,)),
+            pltpu.VMEM((2, dh, dh), BF),
+            pltpu.VMEM((3, 2, half, slab, dh), BF),
+            pltpu.VMEM((nz + 1, slab, dh), BF),
+            pltpu.VMEM((slab, dh), BF),
+            pltpu.VMEM((nz, 2, dh), F32),
+            pltpu.VMEM((2, dh), F32),
+            pltpu.VMEM((2, dh), F32),
+            dma((4,)), dma((2, n_dp)), dma((2, n_dp)), dma((2, n_dp)), dma((2, n_dp)), dma((3, 2, half)), dma((2,)),
             dma((blocks, 2)), dma((blocks, 2)), dma((blocks, 2)), dma((blocks, 2)),
             dma((2, blocks)), dma((2, blocks)), dma((2, blocks)), dma((2, blocks)),
             dma((2, blocks)), dma((blocks,)), dma((blocks,)), dma((blocks,)), dma((2, blocks)), dma((blocks,)), dma((2,)),
+            dma((3, 2, half)), dma((3, 2, half)), dma((nz + 1,)), dma((nz + 1,)), dma((2, half)), dma((2, half)), dma((2,)),
         ],
         compiler_params=pltpu.CompilerParams(
             collective_id=0, has_side_effects=True, vmem_limit_bytes=60 * 1024 * 1024
         ),
         name="relay",
-    )(out_pair.astype(BF), out_grad, f_weight, g_weight, gains)
-    summed = lax.psum_scatter(part, "dp", scatter_dimension=0, tiled=True).astype(F32)
-    gain = lax.psum(gain, "dp")
-    return pair, grad, summed[None, :, :dh], summed[None, :, dh:], gain
+    )(out_pair, out_grad, f_weight, g_weight, gains)
 
 
 def solution(mesh):

time: 294 us -> 242 us (0.82)
  the two profiles are of different devices: /device:TPU:16 before, /device:TPU:1 now
where the time goes in v2:
time: 242 us
  Pallas kernels  235 us (97%)
  local copies, waits for them, and re-layouts  5.8 us (2%)
    pallas_call x1, Pallas kernels, shards(): pl.pallas_call(functools.partial(relay_kernel, n_section, n_dp), out_shap...  235 us
    unnamed x13, local copies, waits for them, and re-layouts  5.8 us

profile of v2, /device:TPU:1, one launch (start us, length us, event | category | flops | bytes accessed | tf_op | source)
XLA Modules:
  0.0 241.6 jit_solution(15422585209296553424)
XLA Ops:
  0.6 235.2 %relay.1 = (f32[1,128,2048]{2,1,0:T(8,128)}, bf16[1,128,2048]{2,1,0:T(8,128)(2,1)}, f32[1,64,1024]{2,1,0:T(8,128)}, f32[1,64,1024]{2,1,0:T(8,128)}, f32[1,2,1024]{2,1,0:T(2,128)}) custom-call(f32[128,2048]{1,0:T(8,128)} %top_pair.1, bf16[128,2048]{1,0:T(8,128)(2,1)} %top_grad.1, bf16[1,64,1024]{2,1,0:T(8,128)(2,1)} %f_own.1, bf16[1,64,1024]{2,1,0:T(8,128)(2,1)} %g_own.1, ...), custom_call_target="tpu_custom_call" | custom-call | tf_op jit(solution)/shard_map/relay/pallas_call | solution.py:497
  235.8 0.0 copy-start
  235.8 2.4 copy.15
  238.2 0.0 copy-done
  238.2 0.0 copy-start.2
  238.2 0.8 copy.16
  239.0 0.3 copy-done.2
  239.3 0.0 copy-start.1
  239.3 0.7 copy.17
  240.0 0.3 copy-done.1
  240.3 0.0 copy-start.3
  240.3 0.7 copy.18
  241.0 0.0 copy-done.3
  241.0 0.6 copy.19
Async XLA Ops:
  235.8 2.4 copy-start
  238.2 1.1 copy-start.2
  239.3 1.0 copy-start.1
  240.3 0.7 copy-start.3
